TPU v7x, 32 devices: a whole 2x2x4 slice. The times are simulated.
32 devices in a mesh: outer: 4 (over z), inner: 8 (over y, x, core).
Axes of the slice: x: 2, y: 2, z: 4, core: 2. Of those that a mesh axis runs over, the one named last changes fastest.
Arguments:
- query_proj: bfloat16 [2048, 8192], P(('outer', 'inner')), may hold values from -8 to 8
- key_proj: bfloat16 [2048, 512], P(('outer', 'inner')), may hold values from -8 to 8
- value_proj: bfloat16 [2048, 512], P(('outer', 'inner')), may hold values from -6 to 6
- positions: int32 [2048], P(('outer', 'inner')), may hold values from 0 to 2047, each once
Outputs:
- attended: bfloat16 [2048, 8192], P(('outer', 'inner'))
Inputs may be any that keep to these rules, and one draw needn't show every extreme that they name: `positions`: each position from 0 to 2047 appears exactly once.
All inputs are finite; a program needn't handle non-finite values.
Results may differ from a plain program's by a relative error of at most 0.005.
Values may be sent and summed in bfloat16 or wider, within the bound.
A program may use at most 64 MiB of HBM per device.

v0:
```python
import math
import jax
import jax.numpy as jnp
from jax import lax
from jax.sharding import PartitionSpec as P

HEAD_WIDTH = 128
masked_score = -1e30


def update(carried, key_value_block, key_pos, query_cluster, query_pos):
    running_top, running_sum, accumulated = carried
    heads_kv = query_cluster.shape[0]
    head_dim = query_cluster.shape[2]
    width = heads_kv * head_dim
    rows_kv = key_value_block.shape[0]
    key_slice = key_value_block[:, :width].reshape(rows_kv, heads_kv, head_dim)
    value_slice = key_value_block[:, width:].reshape(rows_kv, heads_kv, head_dim)
    scores = jnp.einsum(
        "lva,vga->vlg", key_slice, query_cluster, preferred_element_type=jnp.float32
    ) * (1.0 / math.sqrt(head_dim))
    visible = key_pos[None, :, None] <= query_pos[None, None, :]
    block_top = jnp.max(jnp.where(visible, scores, masked_score), axis=1)
    new_top = jnp.maximum(running_top, block_top)
    softmax_weights = jnp.where(visible, jnp.exp(scores - new_top[:, None, :]), 0.0)
    rescale = jnp.exp(running_top - new_top)
    running_sum = running_sum * rescale + jnp.sum(softmax_weights, axis=1)
    accumulated = accumulated * rescale[:, :, None] + jnp.einsum(
        "goi,ogt->git",
        softmax_weights.astype(jnp.bfloat16),
        value_slice,
        preferred_element_type=jnp.float32,
    )
    return (new_top, running_sum, accumulated)


def make_folder(query_cluster, query_pos):

    def fold_piece(carried, kv_piece, first_row):
        kv_rows, key_pos = kv_piece
        row_count = kv_rows.shape[0]
        sub_rows = math.gcd(row_count, 512)
        stacked = kv_rows.reshape(row_count // sub_rows, sub_rows, kv_rows.shape[1])
        pos_stack = key_pos.reshape(row_count // sub_rows, sub_rows)

        def inner_step(carry_in, sub_block):
            return (update(carry_in, sub_block[0], sub_block[1], query_cluster, query_pos), None)

        carried, unused = lax.scan(inner_step, carried, (stacked, pos_stack))
        return carried

    return fold_piece


def start_state(heads_kv, query_rows, head_dim):
    return (
        jnp.full((heads_kv, query_rows), masked_score, jnp.float32),
        jnp.zeros((heads_kv, query_rows), jnp.float32),
        jnp.zeros((heads_kv, query_rows, head_dim), jnp.float32),
    )


def finish(carried):
    return carried[2] / carried[1][:, :, None]


def body(query_proj, key_proj, value_proj, positions):
    tok_rows = query_proj.shape[0]
    head_dim = HEAD_WIDTH
    heads_all = query_proj.shape[1] // head_dim
    heads_kv = key_proj.shape[1] // head_dim
    group_size = heads_all // heads_kv
    inner_count = lax.axis_size("inner")
    per_device = heads_all // inner_count
    repeat_count = group_size // per_device
    key_spread = jnp.repeat(key_proj.reshape(tok_rows, heads_kv, head_dim), repeat_count, axis=1)
    value_broadcast = jnp.repeat(
        value_proj.reshape(tok_rows, heads_kv, head_dim), repeat_count, axis=1
    )
    kv_spread = jnp.concatenate([key_spread, value_broadcast], axis=2).reshape(
        tok_rows, inner_count * 2 * head_dim
    )
    query_heads, kv_heads = (
        lax.all_to_all(query_proj, "inner", split_axis=1, concat_axis=0, tiled=True),
        lax.all_to_all(kv_spread, "inner", split_axis=1, concat_axis=0, tiled=True),
    )
    group_pos = lax.all_gather(positions, "inner", axis=0, tiled=True)
    group_rows = query_heads.shape[0]
    query_cluster = (
        query_heads.reshape(group_rows, per_device, head_dim)
        .transpose(1, 0, 2)
        .reshape(1, per_device * group_rows, head_dim)
    )
    query_pos = jnp.tile(group_pos, per_device)
    folder = make_folder(query_cluster, query_pos)
    initial = start_state(1, per_device * group_rows, head_dim)
    carried = folder(
        initial,
        (
            lax.all_gather(kv_heads, "outer", axis=0, tiled=True),
            lax.all_gather(group_pos, "outer", axis=0, tiled=True),
        ),
        jnp.int32(0),
    )
    result = (
        finish(carried)
        .reshape(per_device, group_rows, head_dim)
        .transpose(1, 0, 2)
        .reshape(group_rows, per_device * head_dim)
        .astype(jnp.bfloat16)
    )
    return lax.all_to_all(result, "inner", split_axis=0, concat_axis=1, tiled=True)


def solution(mesh):
    return jax.shard_map(
        body,
        mesh=mesh,
        in_specs=(
            P(("outer", "inner"), None),
            P(("outer", "inner"), None),
            P(("outer", "inner"), None),
            P(("outer", "inner")),
        ),
        out_specs=P(("outer", "inner"), None),
        check_vma=False,
    )
```

profile of v0, /device:TPU:0, one launch (start us, length us, event | category | flops | bytes accessed | tf_op | source)
XLA Modules:
  0.0 115.0 jit_solution(7399036608634765369)
XLA Ops:
  6.5 0.0 copy-start
  6.5 0.0 all-gather.3.cloned.1.call-start
  6.5 0.8 copy-done
  7.4 0.9 copy_bitcast_fusion.2
  8.3 12.0 %all_to_all.48 = bf16[64,8,256]{2,0,1:T(8,128)(2,1)} all-to-all(bf16[64,8,256]{2,0,1:T(8,128)(2,1)S(1)} %pad_maximum_fusion), channel_id=1, replica_groups=mesh['outer'=4,'inner'=8] {'inner'}, dimensions={1} | all-to-all | bytes 524288 | tf_op jit(solution)/shard_map/all_to_all | solution.py:85
  20.3 0.0 all-gather.3.cloned.1.call-update
  20.4 2.3 %copy.35 = bf16[8,8,8,1024]{3,2,0,1:T(8,128)(2,1)} copy(bf16[8,8,8,1024]{3,2,1,0:T(8,128)(2,1)} %bitcast.91) | data formatting | bytes 2097152 | tf_op jit(solution)/shard_map/all_to_all | solution.py:84
  22.7 3.6 %all-to-all-start.1 = ((bf16[64,8,1024]{2,0,1:T(8,128)(2,1)}), bf16[64,8,1024]{2,0,1:T(8,128)(2,1)S(1)}, u32[]{:S(2)}, u32[]{:S(2)}) async-start(bf16[64,8,1024]{2,0,1:T(8,128)(2,1)} %bitcast.56), calls=%async_computation.1 | async-start | bytes 2097152 | tf_op jit(solution)/shard_map/all_to_all | solution.py:84
  26.3 1.3 %dynamic-slice = u32[1]{0:T(128)} dynamic-slice(u32[32]{0:T(128)} %constant.26, u32[]{:T(128)S(6)} %add.9), dynamic_slice_sizes={1} | dynamic-slice | bytes 12
  28.3 0.9 dynamic-update-slice
  29.1 14.7 %all-reduce = s32[512]{0:T(512)S(1)} all-reduce(s32[512]{0:T(512)S(1)} %dynamic-update-slice), channel_id=1, replica_groups=mesh['outer'=4,'inner'=8] {'inner'}, use_global_device_ids=true, to_apply=%add | all-reduce | flops 512 | bytes 4096
  43.8 12.1 %all-gather = s32[4,1,512]{2,1,0:T(1,128)S(1)} all-gather(s32[1,1,512]{2,1,0:T(1,128)S(1)} %bitcast.102), channel_id=1, replica_groups=mesh['outer'=4,'inner'=8] {'outer'}, dimensions={0}, use_global_device_ids=true | all-gather | bytes 10240 | tf_op jit(solution)/shard_map/all_gather | solution.py:101
  55.9 0.0 all-to-all-done.1
  55.9 0.3 copy.29
  56.2 0.1 copy.20
  56.4 0.0 all-gather.3.cloned.1.call-done
  56.4 31.0 %while.15 = (s32[]{:T(128)}, f32[1,4096]{1,0:T(1,128)S(1)}, f32[1,4096]{1,0:T(1,128)S(1)}, f32[1,4096,128]{2,1,0:T(8,128)S(1)}, s32[4,512]{1,0:T(4,128)S(1)}, /*...) while((s32[]{:T(128)}, f32[1,4096]{1,0:T(1,128)S(1)}, ...), condition=%wide.region_3.4_spmd.clone, body=%wide.region_0.3_spmd.clone.sunk | while | flops 1104695296 | bytes 31568000 | solution.py:49
  56.5 1.0 dynamic-slice_bitcast_fusion.2
  57.4 1.4 %fusion.31 = (f32[4096]{0:T(1024)S(1)}, f32[512,4096]{1,0:T(8,128)S(1)}) fusion(s32[4096]{0:T(1024)S(1)} %bitcast.86, s32[512]{0:T(512)S(1)} %bitcast.99, bf16[1,4096,128]{2,1,0:T(8,128)(2,1)S(1)} %get-tuple-element.183, bf16[512,256]{1,0:T(8,128)(2,1)S(1)} %dynamic-slice_bitcast_fusion.2), kind=kOutput, calls=%fused_computation.3.clone.1 | convolution fusion | flops 545255424 | bytes 9603072 | tf_op jit(solution)/shard_map/while/body/eval_jaxpr/lva,vga->vlg/dot_general | solution.py:19
  58.9 2.2 %fusion.33 = f32[4096]{0:T(1024)S(1)} fusion(f32[512,4096]{1,0:T(8,128)S(1)} %get-tuple-element.154, f32[4096]{0:T(1024)S(1)} %bitcast.79, s32[4096]{0:T(1024)S(1)} %bitcast.87, s32[512]{0:T(512)S(1)} %bitcast.100), kind=kLoop, calls=%fused_computation.5.clone.1 | loop fusion | flops 10481664 | bytes 8439808 | tf_op jit(solution)/shard_map/while/body/eval_jaxpr/reduce_sum | solution.py:27
  61.1 0.1 fusion.34
  61.2 3.0 %fusion.35 = f32[1,4096,128]{2,1,0:T(8,128)S(1)} fusion(f32[512,4096]{1,0:T(8,128)S(1)} %get-tuple-element.154, f32[4096]{0:T(1024)S(1)} %bitcast.80, s32[4096]{0:T(1024)S(1)} %bitcast.88, s32[512]{0:T(512)S(1)} %bitcast.101, f32[1,4096,128]{2,1,0:T(8,128)S(1)} %get-tuple-element.170, f32[4096]{0:T(1024)S(1)} %bitcast.98, pred[]{:T(512)S(6)} %compare.3, ...), kind=kOutput, calls=%fused_computation.7.clone.1 | convolution fusion | flops 548929536 | bytes 12765185 | tf_op jit(solution)/shard_map/while/body/eval_jaxpr/goi,ogt->git/dot_general | solution.py:28
  64.2 1.0 dynamic-slice_bitcast_fusion.2
  65.2 1.4 %fusion.31 = (f32[4096]{0:T(1024)S(1)}, f32[512,4096]{1,0:T(8,128)S(1)}) fusion(s32[4096]{0:T(1024)S(1)} %bitcast.86, s32[512]{0:T(512)S(1)} %bitcast.99, bf16[1,4096,128]{2,1,0:T(8,128)(2,1)S(1)} %get-tuple-element.183, bf16[512,256]{1,0:T(8,128)(2,1)S(1)} %dynamic-slice_bitcast_fusion.2), kind=kOutput, calls=%fused_computation.3.clone.1 | convolution fusion | flops 545255424 | bytes 9603072 | tf_op jit(solution)/shard_map/while/body/eval_jaxpr/lva,vga->vlg/dot_general | solution.py:19
  66.6 2.2 %fusion.33 = f32[4096]{0:T(1024)S(1)} fusion(f32[512,4096]{1,0:T(8,128)S(1)} %get-tuple-element.154, f32[4096]{0:T(1024)S(1)} %bitcast.79, s32[4096]{0:T(1024)S(1)} %bitcast.87, s32[512]{0:T(512)S(1)} %bitcast.100), kind=kLoop, calls=%fused_computation.5.clone.1 | loop fusion | flops 10481664 | bytes 8439808 | tf_op jit(solution)/shard_map/while/body/eval_jaxpr/reduce_sum | solution.py:27
  68.8 0.1 fusion.34
  68.9 3.0 %fusion.35 = f32[1,4096,128]{2,1,0:T(8,128)S(1)} fusion(f32[512,4096]{1,0:T(8,128)S(1)} %get-tuple-element.154, f32[4096]{0:T(1024)S(1)} %bitcast.80, s32[4096]{0:T(1024)S(1)} %bitcast.88, s32[512]{0:T(512)S(1)} %bitcast.101, f32[1,4096,128]{2,1,0:T(8,128)S(1)} %get-tuple-element.170, f32[4096]{0:T(1024)S(1)} %bitcast.98, pred[]{:T(512)S(6)} %compare.3, ...), kind=kOutput, calls=%fused_computation.7.clone.1 | convolution fusion | flops 548929536 | bytes 12765185 | tf_op jit(solution)/shard_map/while/body/eval_jaxpr/goi,ogt->git/dot_general | solution.py:28
  71.9 1.0 dynamic-slice_bitcast_fusion.2
  72.9 1.4 %fusion.31 = (f32[4096]{0:T(1024)S(1)}, f32[512,4096]{1,0:T(8,128)S(1)}) fusion(s32[4096]{0:T(1024)S(1)} %bitcast.86, s32[512]{0:T(512)S(1)} %bitcast.99, bf16[1,4096,128]{2,1,0:T(8,128)(2,1)S(1)} %get-tuple-element.183, bf16[512,256]{1,0:T(8,128)(2,1)S(1)} %dynamic-slice_bitcast_fusion.2), kind=kOutput, calls=%fused_computation.3.clone.1 | convolution fusion | flops 545255424 | bytes 9603072 | tf_op jit(solution)/shard_map/while/body/eval_jaxpr/lva,vga->vlg/dot_general | solution.py:19
  74.4 2.2 %fusion.33 = f32[4096]{0:T(1024)S(1)} fusion(f32[512,4096]{1,0:T(8,128)S(1)} %get-tuple-element.154, f32[4096]{0:T(1024)S(1)} %bitcast.79, s32[4096]{0:T(1024)S(1)} %bitcast.87, s32[512]{0:T(512)S(1)} %bitcast.100), kind=kLoop, calls=%fused_computation.5.clone.1 | loop fusion | flops 10481664 | bytes 8439808 | tf_op jit(solution)/shard_map/while/body/eval_jaxpr/reduce_sum | solution.py:27
  76.6 0.1 fusion.34
  76.7 3.0 %fusion.35 = f32[1,4096,128]{2,1,0:T(8,128)S(1)} fusion(f32[512,4096]{1,0:T(8,128)S(1)} %get-tuple-element.154, f32[4096]{0:T(1024)S(1)} %bitcast.80, s32[4096]{0:T(1024)S(1)} %bitcast.88, s32[512]{0:T(512)S(1)} %bitcast.101, f32[1,4096,128]{2,1,0:T(8,128)S(1)} %get-tuple-element.170, f32[4096]{0:T(1024)S(1)} %bitcast.98, pred[]{:T(512)S(6)} %compare.3, ...), kind=kOutput, calls=%fused_computation.7.clone.1 | convolution fusion | flops 548929536 | bytes 12765185 | tf_op jit(solution)/shard_map/while/body/eval_jaxpr/goi,ogt->git/dot_general | solution.py:28
  79.7 1.0 dynamic-slice_bitcast_fusion.2
  80.7 1.4 %fusion.31 = (f32[4096]{0:T(1024)S(1)}, f32[512,4096]{1,0:T(8,128)S(1)}) fusion(s32[4096]{0:T(1024)S(1)} %bitcast.86, s32[512]{0:T(512)S(1)} %bitcast.99, bf16[1,4096,128]{2,1,0:T(8,128)(2,1)S(1)} %get-tuple-element.183, bf16[512,256]{1,0:T(8,128)(2,1)S(1)} %dynamic-slice_bitcast_fusion.2), kind=kOutput, calls=%fused_computation.3.clone.1 | convolution fusion | flops 545255424 | bytes 9603072 | tf_op jit(solution)/shard_map/while/body/eval_jaxpr/lva,vga->vlg/dot_general | solution.py:19
  82.1 2.2 %fusion.33 = f32[4096]{0:T(1024)S(1)} fusion(f32[512,4096]{1,0:T(8,128)S(1)} %get-tuple-element.154, f32[4096]{0:T(1024)S(1)} %bitcast.79, s32[4096]{0:T(1024)S(1)} %bitcast.87, s32[512]{0:T(512)S(1)} %bitcast.100), kind=kLoop, calls=%fused_computation.5.clone.1 | loop fusion | flops 10481664 | bytes 8439808 | tf_op jit(solution)/shard_map/while/body/eval_jaxpr/reduce_sum | solution.py:27
  84.3 0.1 fusion.34
  84.4 3.0 %fusion.35 = f32[1,4096,128]{2,1,0:T(8,128)S(1)} fusion(f32[512,4096]{1,0:T(8,128)S(1)} %get-tuple-element.154, f32[4096]{0:T(1024)S(1)} %bitcast.80, s32[4096]{0:T(1024)S(1)} %bitcast.88, s32[512]{0:T(512)S(1)} %bitcast.101, f32[1,4096,128]{2,1,0:T(8,128)S(1)} %get-tuple-element.170, f32[4096]{0:T(1024)S(1)} %bitcast.98, pred[]{:T(512)S(6)} %compare.3, ...), kind=kOutput, calls=%fused_computation.7.clone.1 | convolution fusion | flops 548929536 | bytes 12765185 | tf_op jit(solution)/shard_map/while/body/eval_jaxpr/goi,ogt->git/dot_general | solution.py:28
  87.4 0.7 divide_convert_fusion
  88.1 0.7 copy.36
  88.8 0.5 convert_element_type.20
  89.3 17.8 %all_to_all.49 = bf16[8,64,1024]{2,1,0:T(8,128)(2,1)S(1)} all-to-all(bf16[8,64,1024]{2,1,0:T(8,128)(2,1)S(1)} %convert_element_type.20), channel_id=1, replica_groups=mesh['outer'=4,'inner'=8] {'inner'}, dimensions={0} | all-to-all | bytes 2097152 | tf_op jit(solution)/shard_map/all_to_all | solution.py:112
  107.1 1.1 copy.28
  (29 shorter events, 0.3 us)
Async XLA Ops:
  6.5 0.8 copy-start
  6.5 49.9 %all-gather.3.cloned.1.call-start = ((), (), s32[]{:S(2)}) async-start(), calls=%async_computation.3 | async-start | bytes 1310720 | tf_op jit(solution)/shard_map/all_gather | solution.py:100
  22.7 33.3 %all-to-all-start.1 = ((bf16[64,8,1024]{2,0,1:T(8,128)(2,1)}), bf16[64,8,1024]{2,0,1:T(8,128)(2,1)S(1)}, u32[]{:S(2)}, u32[]{:S(2)}) async-start(bf16[64,8,1024]{2,0,1:T(8,128)(2,1)} %bitcast.56), calls=%async_computation.1 | async-start | bytes 2097152 | tf_op jit(solution)/shard_map/all_to_all | solution.py:84
Sparse Core Ops, SparseCore 0:
  20.5 27.3 all-gather.2
where the time goes:
time: 116 us; the launch traced here: 115 us
  blocking collectives  56.6 us (49%)
  matrix products  17.6 us (15%)
  between operations  14.2 us (12%)
  local copies, waits for them, and re-layouts  12.8 us (11%)
  other arithmetic  9.87 us (9%)
  starting transfers between devices  3.56 us (3%)
    all_to_all x1, blocking collectives, body(): lax.all_to_all(result, 'inner', split_axis=0, concat_axis=1, tiled=True)  17.8 us
    unnamed x1, blocking collectives  14.7 us
    all_gather x1, blocking collectives, body(): lax.all_gather(group_pos, 'outer', axis=0, tiled=True)  12.1 us
    all_to_all x1, blocking collectives, body(): lax.all_to_all(kv_spread, 'inner', split_axis=1, concat_axis=0, tiled=True)  12 us
    dot_general x4, matrix products, update(): jnp.einsum('goi,ogt->git', softmax_weights.astype(jnp.bfloat16), value_sl...  11.9 us
    reduce_sum x4, other arithmetic, update(): running_sum = running_sum * rescale + jnp.sum(softmax_weights, axis=1)  8.73 us
    dot_general x4, matrix products, update(): jnp.einsum('lva,vga->vlg', key_slice, query_cluster, preferred_element_ty...  5.72 us
    squeeze x4, local copies, waits for them, and re-layouts, fold_piece(): carried, unused = lax.scan(inner_step, carried, (stacked, pos_stack))  3.9 us
  transfers between devices with their start and end apart: 2, of which 0 were waited for; matrix products, arithmetic and copies ran while one was open for 4% of the time, Pallas kernels for 0%

commit v1 on v0

--- a/solution.py
+++ b/solution.py
@@ -81,7 +81,12 @@
         tok_rows, inner_count * 2 * head_dim
     )
     query_heads, kv_heads = (
-        lax.all_to_all(query_proj, "inner", split_axis=1, concat_axis=0, tiled=True),
+        jnp.concatenate(
+            lax.all_to_all(
+                jnp.stack(jnp.split(query_proj, lax.axis_size("inner"), axis=1)), "inner", 0, 0
+            ),
+            axis=0,
+        ),
         lax.all_to_all(kv_spread, "inner", split_axis=1, concat_axis=0, tiled=True),
     )
     group_pos = lax.all_gather(positions, "inner", axis=0, tiled=True)

time: 116 us -> 121 us (1.043)
  blocking collectives: 56.6 us -> 44.7 us
  local copies, waits for them, and re-layouts: 12.8 us -> 23.8 us
  starting transfers between devices: 3.56 us -> 9.39 us
    all_to_all x1 -> x0, blocking collectives: 12 us -> none  [body(): lax.all_to_all(kv_spread, 'inner', split_axis=1, concat_axis=0, tiled=True)]
    unnamed x7 -> x16, local copies, waits for them, and re-layouts: 3.28 us -> 15 us
    all_to_all x1 -> x2, starting transfers between devices: 3.56 us -> 9.35 us  [the longest x1 5.2 us: body(): lax.all_to_all(kv_spread, 'inner', split_axis=1, concat_axis=0, tiled=True)]
    all_to_all x1 -> x0, local copies, waits for them, and re-layouts: 2.29 us -> none  [body(): lax.all_to_all(query_proj, 'inner', split_axis=1, concat_axis=0, tiled=True)]
    another operation x0 -> x2, local copies, waits for them, and re-layouts: none -> 1.71 us  [the longest x1 1.57 us: body(): jnp.stack(jnp.split(query_proj, lax.axis_size('inner'), axis=1))]
  transfers between devices with their start and end apart: 2 -> 3, of which waited for: 0 -> 0; matrix products, arithmetic and copies ran while one was open for 4% -> 13% of each run, Pallas kernels for 0% -> 0%
where the time goes in v1:
time: 121 us
  blocking collectives  44.7 us (37%)
  local copies, waits for them, and re-layouts  23.8 us (20%)
  matrix products  17.6 us (15%)
  between operations  14.2 us (12%)
  other arithmetic  10.6 us (9%)
  starting transfers between devices  9.39 us (8%)
    all_to_all x1, blocking collectives, body(): lax.all_to_all(result, 'inner', split_axis=0, concat_axis=1, tiled=True)  17.8 us
    unnamed x16, local copies, waits for them, and re-layouts  15 us
    unnamed x1, blocking collectives  14.8 us
    all_gather x1, blocking collectives, body(): lax.all_gather(group_pos, 'outer', axis=0, tiled=True)  12.1 us
    dot_general x4, matrix products, update(): jnp.einsum('goi,ogt->git', softmax_weights.astype(jnp.bfloat16), value_sl...  11.9 us
    reduce_sum x4, other arithmetic, update(): running_sum = running_sum * rescale + jnp.sum(softmax_weights, axis=1)  8.73 us
    dot_general x4, matrix products, update(): jnp.einsum('lva,vga->vlg', key_slice, query_cluster, preferred_element_ty...  5.71 us
    all_to_all x1, starting transfers between devices, body(): lax.all_to_all(kv_spread, 'inner', split_axis=1, concat_axis=0, tiled=True)  5.2 us
  transfers between devices with their start and end apart: 3, of which 0 were waited for; matrix products, arithmetic and copies ran while one was open for 13% of the time, Pallas kernels for 0%

profile of v1, /device:TPU:0, one launch (start us, length us, event | category | flops | bytes accessed | tf_op | source)
XLA Modules:
  0.0 120.5 jit_solution(16819064252035802341)
XLA Ops:
  6.5 0.8 copy-done
  7.4 0.9 copy_bitcast_fusion.1
  8.3 0.7 pad_maximum_fusion
  9.0 5.2 %all-to-all-start = ((bf16[64,8,256]{2,0,1:T(8,128)(2,1)}), bf16[64,8,256]{2,0,1:T(8,128)(2,1)S(1)}, u32[]{:S(2)}, u32[]{:S(2)}) async-start(bf16[64,8,256]{2,0,1:T(8,128)(2,1)} %pad_maximum_fusion), calls=%async_computation | async-start | bytes 524288 | tf_op jit(solution)/shard_map/all_to_all | solution.py:90
  14.2 0.0 all-gather.3.cloned.1.call-start
  14.3 1.6 %bitcast_dynamic-update-slice_fusion.7 = bf16[8,64,1024]{2,1,0:T(8,128)(2,1)} fusion(bf16[64,8192]{1,0:T(8,128)(2,1)} %param.6), kind=kLoop, calls=%fused_computation.38 | loop fusion | bytes 262144
  15.8 1.6 %bitcast_dynamic-update-slice_fusion.6 = bf16[8,64,1024]{2,1,0:T(8,128)(2,1)} fusion(bf16[8,64,1024]{2,1,0:T(8,128)(2,1)} %bitcast_dynamic-update-slice_fusion.7, bf16[64,8192]{1,0:T(8,128)(2,1)} %param.6), kind=kLoop, calls=%fused_computation.37 | loop fusion | bytes 262144
  17.4 1.6 %bitcast_dynamic-update-slice_fusion.5 = bf16[8,64,1024]{2,1,0:T(8,128)(2,1)} fusion(bf16[8,64,1024]{2,1,0:T(8,128)(2,1)} %bitcast_dynamic-update-slice_fusion.6, bf16[64,8192]{1,0:T(8,128)(2,1)} %param.6), kind=kLoop, calls=%fused_computation.36 | loop fusion | bytes 262144
  19.0 1.6 %bitcast_dynamic-update-slice_fusion.4 = bf16[8,64,1024]{2,1,0:T(8,128)(2,1)} fusion(bf16[8,64,1024]{2,1,0:T(8,128)(2,1)} %bitcast_dynamic-update-slice_fusion.5, bf16[64,8192]{1,0:T(8,128)(2,1)} %param.6), kind=kLoop, calls=%fused_computation.35 | loop fusion | bytes 262144
  20.5 1.6 %bitcast_dynamic-update-slice_fusion.3 = bf16[8,64,1024]{2,1,0:T(8,128)(2,1)} fusion(bf16[8,64,1024]{2,1,0:T(8,128)(2,1)} %bitcast_dynamic-update-slice_fusion.4, bf16[64,8192]{1,0:T(8,128)(2,1)} %param.6), kind=kLoop, calls=%fused_computation.34 | loop fusion | bytes 262144
  22.1 0.7 copy-done.1
  22.8 1.6 %bitcast_dynamic-update-slice_fusion.2 = bf16[8,64,1024]{2,1,0:T(8,128)(2,1)} fusion(bf16[8,64,1024]{2,1,0:T(8,128)(2,1)} %bitcast_dynamic-update-slice_fusion.3, bf16[64,8192]{1,0:T(8,128)(2,1)} %param.6), kind=kLoop, calls=%fused_computation.33 | loop fusion | bytes 262144
  24.4 1.6 %bitcast_dynamic-update-slice_fusion.1 = bf16[8,64,1024]{2,1,0:T(8,128)(2,1)} fusion(bf16[8,64,1024]{2,1,0:T(8,128)(2,1)} %bitcast_dynamic-update-slice_fusion.2, bf16[64,8192]{1,0:T(8,128)(2,1)} %param.6), kind=kLoop, calls=%fused_computation.32 | loop fusion | bytes 262144
  26.0 1.6 %bitcast_dynamic-update-slice_fusion = bf16[8,64,1024]{2,1,0:T(8,128)(2,1)} fusion(bf16[8,64,1024]{2,1,0:T(8,128)(2,1)} %bitcast_dynamic-update-slice_fusion.1, bf16[64,8192]{1,0:T(8,128)(2,1)} %param.6), kind=kLoop, calls=%fused_computation.31 | loop fusion | bytes 262144 | tf_op jit(solution)/shard_map/stack | solution.py:86
  27.5 4.2 %all-to-all-start.1 = ((bf16[8,64,1024]{2,1,0:T(8,128)(2,1)}), bf16[8,64,1024]{2,1,0:T(8,128)(2,1)S(1)}, u32[]{:S(2)}, u32[]{:S(2)}) async-start(bf16[8,64,1024]{2,1,0:T(8,128)(2,1)} %bitcast_dynamic-update-slice_fusion), calls=%async_computation.1 | async-start | bytes 2097152 | tf_op jit(solution)/shard_map/all_to_all | solution.py:85
  31.7 1.3 %dynamic-slice = u32[1]{0:T(128)} dynamic-slice(u32[32]{0:T(128)} %constant.26, u32[]{:T(128)S(6)} %add.9), dynamic_slice_sizes={1} | dynamic-slice | bytes 12
  33.7 0.9 dynamic-update-slice
  34.5 14.8 %all-reduce = s32[512]{0:T(512)S(1)} all-reduce(s32[512]{0:T(512)S(1)} %dynamic-update-slice), channel_id=1, replica_groups=mesh['outer'=4,'inner'=8] {'inner'}, use_global_device_ids=true, to_apply=%add | all-reduce | flops 512 | bytes 4096
  49.3 12.1 %all-gather = s32[4,1,512]{2,1,0:T(1,128)S(1)} all-gather(s32[1,1,512]{2,1,0:T(1,128)S(1)} %bitcast.112), channel_id=1, replica_groups=mesh['outer'=4,'inner'=8] {'outer'}, dimensions={0}, use_global_device_ids=true | all-gather | bytes 10240 | tf_op jit(solution)/shard_map/all_gather | solution.py:106
  61.5 0.3 copy.27
  61.8 0.1 copy.19
  61.9 0.0 all-gather.3.cloned.1.call-done
  61.9 31.0 %while.15 = (s32[]{:T(128)}, f32[1,4096]{1,0:T(1,128)S(1)}, f32[1,4096]{1,0:T(1,128)S(1)}, f32[1,4096,128]{2,1,0:T(8,128)S(1)}, s32[4,512]{1,0:T(4,128)S(1)}, /*...) while((s32[]{:T(128)}, f32[1,4096]{1,0:T(1,128)S(1)}, ...), condition=%wide.region_3.4_spmd.clone, body=%wide.region_0.3_spmd.clone.sunk | while | flops 1104695296 | bytes 31568000 | solution.py:49
  62.0 1.0 dynamic-slice_bitcast_fusion.2
  63.0 1.4 %fusion.31 = (f32[4096]{0:T(1024)S(1)}, f32[512,4096]{1,0:T(8,128)S(1)}) fusion(s32[4096]{0:T(1024)S(1)} %bitcast.97, s32[512]{0:T(512)S(1)} %bitcast.109, bf16[1,4096,128]{2,1,0:T(8,128)(2,1)S(1)} %get-tuple-element.183, bf16[512,256]{1,0:T(8,128)(2,1)S(1)} %dynamic-slice_bitcast_fusion.2), kind=kOutput, calls=%fused_computation.3.clone.1 | convolution fusion | flops 545255424 | bytes 9603072 | tf_op jit(solution)/shard_map/while/body/eval_jaxpr/lva,vga->vlg/dot_general | solution.py:19
  64.4 2.2 %fusion.33 = f32[4096]{0:T(1024)S(1)} fusion(f32[512,4096]{1,0:T(8,128)S(1)} %get-tuple-element.154, f32[4096]{0:T(1024)S(1)} %bitcast.90, s32[4096]{0:T(1024)S(1)} %bitcast.98, s32[512]{0:T(512)S(1)} %bitcast.110), kind=kLoop, calls=%fused_computation.5.clone.1 | loop fusion | flops 10481664 | bytes 8439808 | tf_op jit(solution)/shard_map/while/body/eval_jaxpr/reduce_sum | solution.py:27
  66.6 0.1 fusion.34
  66.7 3.0 %fusion.35 = f32[1,4096,128]{2,1,0:T(8,128)S(1)} fusion(f32[512,4096]{1,0:T(8,128)S(1)} %get-tuple-element.154, f32[4096]{0:T(1024)S(1)} %bitcast.91, s32[4096]{0:T(1024)S(1)} %bitcast.99, s32[512]{0:T(512)S(1)} %bitcast.111, f32[1,4096,128]{2,1,0:T(8,128)S(1)} %get-tuple-element.170, f32[4096]{0:T(1024)S(1)} %bitcast.108, pred[]{:T(512)S(6)} %compare.3, ...), kind=kOutput, calls=%fused_computation.7.clone.1 | convolution fusion | flops 548929536 | bytes 12765185 | tf_op jit(solution)/shard_map/while/body/eval_jaxpr/goi,ogt->git/dot_general | solution.py:28
  69.7 1.0 dynamic-slice_bitcast_fusion.2
  70.7 1.4 %fusion.31 = (f32[4096]{0:T(1024)S(1)}, f32[512,4096]{1,0:T(8,128)S(1)}) fusion(s32[4096]{0:T(1024)S(1)} %bitcast.97, s32[512]{0:T(512)S(1)} %bitcast.109, bf16[1,4096,128]{2,1,0:T(8,128)(2,1)S(1)} %get-tuple-element.183, bf16[512,256]{1,0:T(8,128)(2,1)S(1)} %dynamic-slice_bitcast_fusion.2), kind=kOutput, calls=%fused_computation.3.clone.1 | convolution fusion | flops 545255424 | bytes 9603072 | tf_op jit(solution)/shard_map/while/body/eval_jaxpr/lva,vga->vlg/dot_general | solution.py:19
  72.2 2.2 %fusion.33 = f32[4096]{0:T(1024)S(1)} fusion(f32[512,4096]{1,0:T(8,128)S(1)} %get-tuple-element.154, f32[4096]{0:T(1024)S(1)} %bitcast.90, s32[4096]{0:T(1024)S(1)} %bitcast.98, s32[512]{0:T(512)S(1)} %bitcast.110), kind=kLoop, calls=%fused_computation.5.clone.1 | loop fusion | flops 10481664 | bytes 8439808 | tf_op jit(solution)/shard_map/while/body/eval_jaxpr/reduce_sum | solution.py:27
  74.4 0.1 fusion.34
  74.4 3.0 %fusion.35 = f32[1,4096,128]{2,1,0:T(8,128)S(1)} fusion(f32[512,4096]{1,0:T(8,128)S(1)} %get-tuple-element.154, f32[4096]{0:T(1024)S(1)} %bitcast.91, s32[4096]{0:T(1024)S(1)} %bitcast.99, s32[512]{0:T(512)S(1)} %bitcast.111, f32[1,4096,128]{2,1,0:T(8,128)S(1)} %get-tuple-element.170, f32[4096]{0:T(1024)S(1)} %bitcast.108, pred[]{:T(512)S(6)} %compare.3, ...), kind=kOutput, calls=%fused_computation.7.clone.1 | convolution fusion | flops 548929536 | bytes 12765185 | tf_op jit(solution)/shard_map/while/body/eval_jaxpr/goi,ogt->git/dot_general | solution.py:28
  77.5 1.0 dynamic-slice_bitcast_fusion.2
  78.5 1.4 %fusion.31 = (f32[4096]{0:T(1024)S(1)}, f32[512,4096]{1,0:T(8,128)S(1)}) fusion(s32[4096]{0:T(1024)S(1)} %bitcast.97, s32[512]{0:T(512)S(1)} %bitcast.109, bf16[1,4096,128]{2,1,0:T(8,128)(2,1)S(1)} %get-tuple-element.183, bf16[512,256]{1,0:T(8,128)(2,1)S(1)} %dynamic-slice_bitcast_fusion.2), kind=kOutput, calls=%fused_computation.3.clone.1 | convolution fusion | flops 545255424 | bytes 9603072 | tf_op jit(solution)/shard_map/while/body/eval_jaxpr/lva,vga->vlg/dot_general | solution.py:19
  79.9 2.2 %fusion.33 = f32[4096]{0:T(1024)S(1)} fusion(f32[512,4096]{1,0:T(8,128)S(1)} %get-tuple-element.154, f32[4096]{0:T(1024)S(1)} %bitcast.90, s32[4096]{0:T(1024)S(1)} %bitcast.98, s32[512]{0:T(512)S(1)} %bitcast.110), kind=kLoop, calls=%fused_computation.5.clone.1 | loop fusion | flops 10481664 | bytes 8439808 | tf_op jit(solution)/shard_map/while/body/eval_jaxpr/reduce_sum | solution.py:27
  82.1 0.1 fusion.34
  82.2 3.0 %fusion.35 = f32[1,4096,128]{2,1,0:T(8,128)S(1)} fusion(f32[512,4096]{1,0:T(8,128)S(1)} %get-tuple-element.154, f32[4096]{0:T(1024)S(1)} %bitcast.91, s32[4096]{0:T(1024)S(1)} %bitcast.99, s32[512]{0:T(512)S(1)} %bitcast.111, f32[1,4096,128]{2,1,0:T(8,128)S(1)} %get-tuple-element.170, f32[4096]{0:T(1024)S(1)} %bitcast.108, pred[]{:T(512)S(6)} %compare.3, ...), kind=kOutput, calls=%fused_computation.7.clone.1 | convolution fusion | flops 548929536 | bytes 12765185 | tf_op jit(solution)/shard_map/while/body/eval_jaxpr/goi,ogt->git/dot_general | solution.py:28
  85.2 1.0 dynamic-slice_bitcast_fusion.2
  86.2 1.4 %fusion.31 = (f32[4096]{0:T(1024)S(1)}, f32[512,4096]{1,0:T(8,128)S(1)}) fusion(s32[4096]{0:T(1024)S(1)} %bitcast.97, s32[512]{0:T(512)S(1)} %bitcast.109, bf16[1,4096,128]{2,1,0:T(8,128)(2,1)S(1)} %get-tuple-element.183, bf16[512,256]{1,0:T(8,128)(2,1)S(1)} %dynamic-slice_bitcast_fusion.2), kind=kOutput, calls=%fused_computation.3.clone.1 | convolution fusion | flops 545255424 | bytes 9603072 | tf_op jit(solution)/shard_map/while/body/eval_jaxpr/lva,vga->vlg/dot_general | solution.py:19
  87.7 2.2 %fusion.33 = f32[4096]{0:T(1024)S(1)} fusion(f32[512,4096]{1,0:T(8,128)S(1)} %get-tuple-element.154, f32[4096]{0:T(1024)S(1)} %bitcast.90, s32[4096]{0:T(1024)S(1)} %bitcast.98, s32[512]{0:T(512)S(1)} %bitcast.110), kind=kLoop, calls=%fused_computation.5.clone.1 | loop fusion | flops 10481664 | bytes 8439808 | tf_op jit(solution)/shard_map/while/body/eval_jaxpr/reduce_sum | solution.py:27
  89.9 0.1 fusion.34
  89.9 3.0 %fusion.35 = f32[1,4096,128]{2,1,0:T(8,128)S(1)} fusion(f32[512,4096]{1,0:T(8,128)S(1)} %get-tuple-element.154, f32[4096]{0:T(1024)S(1)} %bitcast.91, s32[4096]{0:T(1024)S(1)} %bitcast.99, s32[512]{0:T(512)S(1)} %bitcast.111, f32[1,4096,128]{2,1,0:T(8,128)S(1)} %get-tuple-element.170, f32[4096]{0:T(1024)S(1)} %bitcast.108, pred[]{:T(512)S(6)} %compare.3, ...), kind=kOutput, calls=%fused_computation.7.clone.1 | convolution fusion | flops 548929536 | bytes 12765185 | tf_op jit(solution)/shard_map/while/body/eval_jaxpr/goi,ogt->git/dot_general | solution.py:28
  92.9 0.7 divide_convert_fusion
  93.7 0.7 copy.32
  94.3 0.5 convert_element_type.20
  94.8 17.8 %all_to_all.37 = bf16[8,64,1024]{2,1,0:T(8,128)(2,1)S(1)} all-to-all(bf16[8,64,1024]{2,1,0:T(8,128)(2,1)S(1)} %convert_element_type.20), channel_id=1, replica_groups=mesh['outer'=4,'inner'=8] {'inner'}, dimensions={0} | all-to-all | bytes 2097152 | tf_op jit(solution)/shard_map/all_to_all | solution.py:117
  112.6 1.1 copy.26
  (33 shorter events, 0.3 us)
Async XLA Ops:
  6.5 0.8 copy-start
  9.0 13.1 %all-to-all-start = ((bf16[64,8,256]{2,0,1:T(8,128)(2,1)}), bf16[64,8,256]{2,0,1:T(8,128)(2,1)S(1)}, u32[]{:S(2)}, u32[]{:S(2)}) async-start(bf16[64,8,256]{2,0,1:T(8,128)(2,1)} %pad_maximum_fusion), calls=%async_computation | async-start | bytes 524288 | tf_op jit(solution)/shard_map/all_to_all | solution.py:90
  14.2 47.7 %all-gather.3.cloned.1.call-start = ((), (), s32[]{:S(2)}) async-start(), calls=%async_computation.3 | async-start | bytes 1310720 | tf_op jit(solution)/shard_map/all_gather | solution.py:105
  22.1 0.7 copy-start.1
  27.5 33.9 %all-to-all-start.1 = ((bf16[8,64,1024]{2,1,0:T(8,128)(2,1)}), bf16[8,64,1024]{2,1,0:T(8,128)(2,1)S(1)}, u32[]{:S(2)}, u32[]{:S(2)}) async-start(bf16[8,64,1024]{2,1,0:T(8,128)(2,1)} %bitcast_dynamic-update-slice_fusion), calls=%async_computation.1 | async-start | bytes 2097152 | tf_op jit(solution)/shard_map/all_to_all | solution.py:85
Sparse Core Ops, SparseCore 0:
  23.0 29.6 all-gather.2
